TPU v7x, 32 devices: a whole 2x2x4 slice. The times are simulated.
32 devices in a mesh: groups: 2 (over x), col: 16 (over z, y, core).
Axes of the slice: x: 2, y: 2, z: 4, core: 2. Of those that a mesh axis runs over, the one named last changes fastest.
Arguments:
- left: bfloat16 [256, 64, 32], P('col', 'groups'), parts along dimension 1, may hold values from -18 to 18
- right: bfloat16 [256, 2560, 32], P('col', 'groups'), parts along dimension 1, may hold values from -18 to 18
- out_weight: bfloat16 [1024, 128], replicated, may hold values from -0.1875 to 0.1875
- out_bias: float32 [128], replicated, may hold values from -3 to 3
Outputs:
- pair_update: bfloat16 [64, 1280, 128], P('groups', 'col'), parts along dimension 0
There are 2 independent parts, one for each index of `groups`. A program takes and returns all parts, laid end to end along the dimension named above; an argument that names none is the same for every part. Nothing has to cross between parts.
All inputs are finite; a program needn't handle non-finite values.
Results may differ from a plain program's by a relative error of at most 0.004.
Values may be sent and summed in bfloat16 or wider, within the bound.
A program may use at most 64 MiB of HBM per device.

v0:
```python
import jax
import jax.numpy as jnp
from jax import lax
from jax.sharding import PartitionSpec as P


def tile_update(left_rows, right_cols, out_weight, out_bias):
    seqs, count, width = left_rows.shape
    columns = right_cols.shape[1]
    outer = (
        jnp.einsum("sic,sje->ijce", left_rows, right_cols, preferred_element_type=jnp.float32)
        / seqs
    )
    flat = outer.astype(jnp.bfloat16).reshape(count * columns, width * width)
    update = jnp.dot(flat, out_weight, preferred_element_type=jnp.float32) + out_bias
    return update.astype(jnp.bfloat16).reshape(count, columns, out_weight.shape[1])


def rows_update(left_rows, right_cols, out_weight, out_bias):
    seqs, count, width = left_rows.shape
    blocks = jnp.transpose(left_rows.reshape(seqs, count // 8, 8, width), (1, 0, 2, 3))
    results = lax.map(lambda block: tile_update(block, right_cols, out_weight, out_bias), blocks)
    return results.reshape(count, right_cols.shape[1], out_weight.shape[1])


def on_device(left, right, out_weight, out_bias):
    left_part, right_cols = (
        lax.all_to_all(left, "col", split_axis=1, concat_axis=0, tiled=True),
        lax.all_to_all(right, "col", split_axis=1, concat_axis=0, tiled=True),
    )
    return rows_update(
        lax.all_gather(left_part, "col", axis=1, tiled=True), right_cols, out_weight, out_bias
    )


def solution(mesh):
    in_specs = (P("col", "groups", None), P("col", "groups", None), P(), P())
    out_specs = P("groups", "col", None)
    return jax.shard_map(
        on_device, mesh=mesh, in_specs=in_specs, out_specs=out_specs, check_vma=False
    )
```

profile of v0, /device:TPU:9, one launch (start us, length us, event | category | flops | bytes accessed | tf_op | source)
XLA Modules:
  0.0 118.3 jit_solution(4670310625103489706)
XLA Ops:
  0.0 1.0 copy.21
  1.0 0.8 reshape.16
  1.7 6.6 %all-to-all-start = ((bf16[16,2,512]{2,1,0:T(2,128)(2,1)}), bf16[16,2,512]{2,1,0:T(2,128)(2,1)S(1)}, u32[]{:S(2)}, u32[]{:S(2)}) async-start(bf16[16,2,512]{2,1,0:T(2,128)(2,1)} %reshape.16), calls=%async_computation | async-start | bytes 65536 | tf_op jit(solution)/shard_map/all_to_all | solution.py:28
  8.3 6.9 %copy.16 = bf16[16,1280,32]{2,0,1:T(8,128)(2,1)} copy(bf16[16,1280,32]{1,2,0:T(8,128)(2,1)} %param.7) | data formatting | bytes 2621440 | tf_op args[1]
  15.2 8.3 %reshape.18 = bf16[16,2,20480]{2,1,0:T(2,128)(2,1)} reshape(bf16[1280,16,32]{2,1,0:T(8,128)(2,1)} %bitcast.49) | data formatting | bytes 2621440
  23.5 6.0 %all-to-all-start.1 = ((bf16[16,2,20480]{2,1,0:T(2,128)(2,1)}), bf16[16,2,20480]{2,1,0:T(2,128)(2,1)S(1)}, u32[]{:S(2)}, u32[]{:S(2)}) async-start(bf16[16,2,20480]{2,1,0:T(2,128)(2,1)} %reshape.18), calls=%async_computation.1 | async-start | bytes 2621440 | tf_op jit(solution)/shard_map/all_to_all | solution.py:29
  29.8 43.8 %all_gather.3 = bf16[256,32,32]{0,2,1:T(8,128)(2,1)} all-gather(bf16[256,2,32]{0,2,1:T(8,128)(2,1)S(1)} %copy.15), channel_id=1, replica_groups=mesh['groups'=2,'col'=16] {'col'}, dimensions={1}, use_global_device_ids=true | all-gather | bytes 557056 | tf_op jit(solution)/shard_map/all_gather | solution.py:32
  73.6 4.0 %reshape.19 = bf16[1280,16,32]{2,1,0:T(8,128)(2,1)} reshape(bf16[16,2,20480]{2,1,0:T(2,128)(2,1)S(1)} %all-to-all-done.1) | data formatting | bytes 2621440
  77.6 6.8 %copy.17 = bf16[16,16,80,32]{2,3,0,1:T(8,128)(2,1)S(1)} copy(bf16[16,16,80,32]{3,0,2,1:T(8,128)(2,1)} %bitcast.48) | data formatting | bytes 2621440 | tf_op jit(solution)/shard_map/all_to_all | solution.py:29
  84.4 1.6 %copy.18 = bf16[256,80,32]{0,1,2:T(8,128)(2,1)S(1)} copy(bf16[256,80,32]{1,2,0:T(8,128)(2,1)S(1)} %bitcast.51) | data formatting | bytes 2621440 | tf_op jit(solution)/shard_map/while | solution.py:22
  86.0 32.3 %while.10 = (s32[]{:T(128)}, bf16[4,8,80,128]{3,2,1,0:T(8,128)(2,1)}, bf16[4,256,8,32]{1,3,2,0:T(8,128)(2,1)}, bf16[256,80,32]{0,1,2:T(8,128)(2,1)S(1)}, bf16[10...) while((s32[]{:T(128)}, bf16[4,8,80,128]{3,2,1,0:T(8,128)(2,1)}, bf16[4,256,8,32]{1,3,2,0:T(8,128)(2,1)}, ...), condition=%wide.region_1.2_spmd, body=%wide.region_0.1_spmd.sunk | while | flops 504791040 | bytes 20547204 | solution.py:22
  86.0 1.1 copy-done
  87.1 1.6 %fusion.18 = bf16[8,80,32,32]{1,2,3,0:T(8,128)(2,1)S(1)} fusion(bf16[256,80,32]{0,1,2:T(8,128)(2,1)S(1)} %get-tuple-element.116, bf16[4,256,8,32]{1,3,2,0:T(8,128)(2,1)} %get-tuple-element.115, s32[]{:T(128)} %get-tuple-element.106), kind=kOutput, calls=%fused_computation.1.clone.1 | convolution fusion | flops 336855040 | bytes 2753024 | tf_op jit(solution)/shard_map/while/body/eval_jaxpr/sic,sje->ijce/dot_general | solution.py:11
  88.7 1.4 %copy.23 = bf16[8,80,32,32]{1,0,3,2:T(8,128)(2,1)S(1)} copy(bf16[8,80,32,32]{1,2,3,0:T(8,128)(2,1)S(1)} %fusion.18) | data formatting | bytes 2621440 | tf_op jit(solution)/shard_map/while/body/eval_jaxpr/convert_element_type | solution.py:14
  90.1 1.7 %reshape.21 = bf16[640,1024]{0,1:T(8,128)(2,1)S(1)} reshape(bf16[8,80,32,32]{1,0,3,2:T(8,128)(2,1)S(1)} %copy.23) | data formatting | bytes 2621440 | tf_op jit(solution)/shard_map/while/body/eval_jaxpr/reshape | solution.py:14
  91.8 1.6 %fusion.19 = bf16[640,128]{1,0:T(8,128)(2,1)S(1)} fusion(bf16[640,1024]{0,1:T(8,128)(2,1)S(1)} %reshape.21, bf16[1024,128]{1,0:T(8,128)(2,1)} %get-tuple-element.117, f32[128]{0:T(128)S(1)} %get-tuple-element.118), kind=kOutput, calls=%fused_computation.4.clone.1 | convolution fusion | flops 167936000 | bytes 1737216 | tf_op jit(solution)/shard_map/while/body/eval_jaxpr/dot_general | solution.py:15
  93.4 0.7 constant_dynamic-update-slice_fusion.2
  94.1 1.1 copy-done
  95.2 1.6 %fusion.18 = bf16[8,80,32,32]{1,2,3,0:T(8,128)(2,1)S(1)} fusion(bf16[256,80,32]{0,1,2:T(8,128)(2,1)S(1)} %get-tuple-element.116, bf16[4,256,8,32]{1,3,2,0:T(8,128)(2,1)} %get-tuple-element.115, s32[]{:T(128)} %get-tuple-element.106), kind=kOutput, calls=%fused_computation.1.clone.1 | convolution fusion | flops 336855040 | bytes 2753024 | tf_op jit(solution)/shard_map/while/body/eval_jaxpr/sic,sje->ijce/dot_general | solution.py:11
  96.8 1.4 %copy.23 = bf16[8,80,32,32]{1,0,3,2:T(8,128)(2,1)S(1)} copy(bf16[8,80,32,32]{1,2,3,0:T(8,128)(2,1)S(1)} %fusion.18) | data formatting | bytes 2621440 | tf_op jit(solution)/shard_map/while/body/eval_jaxpr/convert_element_type | solution.py:14
  98.2 1.7 %reshape.21 = bf16[640,1024]{0,1:T(8,128)(2,1)S(1)} reshape(bf16[8,80,32,32]{1,0,3,2:T(8,128)(2,1)S(1)} %copy.23) | data formatting | bytes 2621440 | tf_op jit(solution)/shard_map/while/body/eval_jaxpr/reshape | solution.py:14
  99.9 1.6 %fusion.19 = bf16[640,128]{1,0:T(8,128)(2,1)S(1)} fusion(bf16[640,1024]{0,1:T(8,128)(2,1)S(1)} %reshape.21, bf16[1024,128]{1,0:T(8,128)(2,1)} %get-tuple-element.117, f32[128]{0:T(128)S(1)} %get-tuple-element.118), kind=kOutput, calls=%fused_computation.4.clone.1 | convolution fusion | flops 167936000 | bytes 1737216 | tf_op jit(solution)/shard_map/while/body/eval_jaxpr/dot_general | solution.py:15
  102.2 1.1 copy-done
  103.2 1.6 %fusion.18 = bf16[8,80,32,32]{1,2,3,0:T(8,128)(2,1)S(1)} fusion(bf16[256,80,32]{0,1,2:T(8,128)(2,1)S(1)} %get-tuple-element.116, bf16[4,256,8,32]{1,3,2,0:T(8,128)(2,1)} %get-tuple-element.115, s32[]{:T(128)} %get-tuple-element.106), kind=kOutput, calls=%fused_computation.1.clone.1 | convolution fusion | flops 336855040 | bytes 2753024 | tf_op jit(solution)/shard_map/while/body/eval_jaxpr/sic,sje->ijce/dot_general | solution.py:11
  104.9 1.4 %copy.23 = bf16[8,80,32,32]{1,0,3,2:T(8,128)(2,1)S(1)} copy(bf16[8,80,32,32]{1,2,3,0:T(8,128)(2,1)S(1)} %fusion.18) | data formatting | bytes 2621440 | tf_op jit(solution)/shard_map/while/body/eval_jaxpr/convert_element_type | solution.py:14
  106.2 1.7 %reshape.21 = bf16[640,1024]{0,1:T(8,128)(2,1)S(1)} reshape(bf16[8,80,32,32]{1,0,3,2:T(8,128)(2,1)S(1)} %copy.23) | data formatting | bytes 2621440 | tf_op jit(solution)/shard_map/while/body/eval_jaxpr/reshape | solution.py:14
  108.0 1.6 %fusion.19 = bf16[640,128]{1,0:T(8,128)(2,1)S(1)} fusion(bf16[640,1024]{0,1:T(8,128)(2,1)S(1)} %reshape.21, bf16[1024,128]{1,0:T(8,128)(2,1)} %get-tuple-element.117, f32[128]{0:T(128)S(1)} %get-tuple-element.118), kind=kOutput, calls=%fused_computation.4.clone.1 | convolution fusion | flops 167936000 | bytes 1737216 | tf_op jit(solution)/shard_map/while/body/eval_jaxpr/dot_general | solution.py:15
  110.2 1.1 copy-done
  111.3 1.6 %fusion.18 = bf16[8,80,32,32]{1,2,3,0:T(8,128)(2,1)S(1)} fusion(bf16[256,80,32]{0,1,2:T(8,128)(2,1)S(1)} %get-tuple-element.116, bf16[4,256,8,32]{1,3,2,0:T(8,128)(2,1)} %get-tuple-element.115, s32[]{:T(128)} %get-tuple-element.106), kind=kOutput, calls=%fused_computation.1.clone.1 | convolution fusion | flops 336855040 | bytes 2753024 | tf_op jit(solution)/shard_map/while/body/eval_jaxpr/sic,sje->ijce/dot_general | solution.py:11
  113.0 1.4 %copy.23 = bf16[8,80,32,32]{1,0,3,2:T(8,128)(2,1)S(1)} copy(bf16[8,80,32,32]{1,2,3,0:T(8,128)(2,1)S(1)} %fusion.18) | data formatting | bytes 2621440 | tf_op jit(solution)/shard_map/while/body/eval_jaxpr/convert_element_type | solution.py:14
  114.3 1.7 %reshape.21 = bf16[640,1024]{0,1:T(8,128)(2,1)S(1)} reshape(bf16[8,80,32,32]{1,0,3,2:T(8,128)(2,1)S(1)} %copy.23) | data formatting | bytes 2621440 | tf_op jit(solution)/shard_map/while/body/eval_jaxpr/reshape | solution.py:14
  116.0 1.6 %fusion.19 = bf16[640,128]{1,0:T(8,128)(2,1)S(1)} fusion(bf16[640,1024]{0,1:T(8,128)(2,1)S(1)} %reshape.21, bf16[1024,128]{1,0:T(8,128)(2,1)} %get-tuple-element.117, f32[128]{0:T(128)S(1)} %get-tuple-element.118), kind=kOutput, calls=%fused_computation.4.clone.1 | convolution fusion | flops 167936000 | bytes 1737216 | tf_op jit(solution)/shard_map/while/body/eval_jaxpr/dot_general | solution.py:15
  (23 shorter events, 2.3 us)
Async XLA Ops:
  1.7 21.8 %all-to-all-start = ((bf16[16,2,512]{2,1,0:T(2,128)(2,1)}), bf16[16,2,512]{2,1,0:T(2,128)(2,1)S(1)}, u32[]{:S(2)}, u32[]{:S(2)}) async-start(bf16[16,2,512]{2,1,0:T(2,128)(2,1)} %reshape.16), calls=%async_computation | async-start | bytes 65536 | tf_op jit(solution)/shard_map/all_to_all | solution.py:28
  23.5 50.1 %all-to-all-start.1 = ((bf16[16,2,20480]{2,1,0:T(2,128)(2,1)}), bf16[16,2,20480]{2,1,0:T(2,128)(2,1)S(1)}, u32[]{:S(2)}, u32[]{:S(2)}) async-start(bf16[16,2,20480]{2,1,0:T(2,128)(2,1)} %reshape.18), calls=%async_computation.1 | async-start | bytes 2621440 | tf_op jit(solution)/shard_map/all_to_all | solution.py:29
  84.4 1.6 %copy-start.2 = (f32[128]{0:T(128)S(1)}, f32[128]{0:T(128)}, u32[]{:S(2)}) copy-start(f32[128]{0:T(128)} %param.9) | copy-start | bytes 1540
  86.0 1.1 copy-start
  91.8 2.3 %copy-start.1 = (bf16[256,80,32]{0,1,2:T(8,128)(2,1)S(1)}, bf16[256,80,32]{0,1,2:T(8,128)(2,1)}, u32[]{:S(2)}) copy-start(bf16[256,80,32]{0,1,2:T(8,128)(2,1)} %copy-done) | copy-start | bytes 3932164 | tf_op jit(solution)/shard_map/while
  94.1 1.1 copy-start
  99.9 2.3 %copy-start.1 = (bf16[256,80,32]{0,1,2:T(8,128)(2,1)S(1)}, bf16[256,80,32]{0,1,2:T(8,128)(2,1)}, u32[]{:S(2)}) copy-start(bf16[256,80,32]{0,1,2:T(8,128)(2,1)} %copy-done) | copy-start | bytes 3932164 | tf_op jit(solution)/shard_map/while
  102.2 1.1 copy-start
  107.9 2.3 %copy-start.1 = (bf16[256,80,32]{0,1,2:T(8,128)(2,1)S(1)}, bf16[256,80,32]{0,1,2:T(8,128)(2,1)}, u32[]{:S(2)}) copy-start(bf16[256,80,32]{0,1,2:T(8,128)(2,1)} %copy-done) | copy-start | bytes 3932164 | tf_op jit(solution)/shard_map/while
  110.2 1.1 copy-start
  116.0 2.3 %copy-start.1 = (bf16[256,80,32]{0,1,2:T(8,128)(2,1)S(1)}, bf16[256,80,32]{0,1,2:T(8,128)(2,1)}, u32[]{:S(2)}) copy-start(bf16[256,80,32]{0,1,2:T(8,128)(2,1)} %copy-done) | copy-start | bytes 3932164 | tf_op jit(solution)/shard_map/while
where the time goes:
time: 119 us; the launch traced here: 118 us
  local copies, waits for them, and re-layouts  48.7 us (41%)
  blocking collectives  43.8 us (37%)
  matrix products  12.9 us (11%)
  starting transfers between devices  12.6 us (11%)
    all_gather x1, blocking collectives, on_device(): lax.all_gather(left_part, 'col', axis=1, tiled=True)  43.8 us
    unnamed x8, local copies, waits for them, and re-layouts  21.1 us
    reshape x4, local copies, waits for them, and re-layouts, tile_update(): flat = outer.astype(jnp.bfloat16).reshape(count * columns, width * width)  6.79 us
    all_to_all x1, local copies, waits for them, and re-layouts, on_device(): lax.all_to_all(right, 'col', split_axis=1, concat_axis=0, tiled=True)  6.76 us
    all_to_all x1, starting transfers between devices, on_device(): lax.all_to_all(left, 'col', split_axis=1, concat_axis=0, tiled=True)  6.58 us
    dot_general x4, matrix products, tile_update(): jnp.einsum('sic,sje->ijce', left_rows, right_cols, preferred_element_type...  6.53 us
    dot_general x4, matrix products, tile_update(): jnp.dot(flat, out_weight, preferred_element_type=jnp.float32) + out_bias  6.39 us
    all_to_all x1, starting transfers between devices, on_device(): lax.all_to_all(right, 'col', split_axis=1, concat_axis=0, tiled=True)  6.02 us
  transfers between devices with their start and end apart: 2, of which 0 were waited for; matrix products, arithmetic and copies ran while one was open for 13% of the time, Pallas kernels for 0%

commit v1 on v0

--- a/solution.py
+++ b/solution.py
@@ -2,6 +2,25 @@
 import jax.numpy as jnp
 from jax import lax
 from jax.sharding import PartitionSpec as P
+
+
+def check_the_rings(values, on_dim, dim_i):
+    local_part, f_next = (lax.axis_size("col"), lax.axis_index("col"))
+    high = values.shape[on_dim] // local_part
+    f_now = jnp.roll(values, -f_next * high, axis=on_dim)
+    seen = [lax.slice_in_dim(f_now, 0, high, axis=on_dim)]
+    for i in range(1, local_part):
+        b_now = lax.slice_in_dim(f_now, i * high, (i + 1) * high, axis=on_dim)
+        seen.append(
+            lax.ppermute(
+                b_now,
+                axis_name="col",
+                perm=[(no, (no + i) % local_part) for no in range(local_part)],
+            )
+        )
+    return jnp.roll(
+        jnp.concatenate(seen[::-1], axis=dim_i), (f_next + 1) * seen[0].shape[dim_i], axis=dim_i
+    )
 
 
 def tile_update(left_rows, right_cols, out_weight, out_bias):
@@ -26,7 +45,7 @@
 def on_device(left, right, out_weight, out_bias):
     left_part, right_cols = (
         lax.all_to_all(left, "col", split_axis=1, concat_axis=0, tiled=True),
-        lax.all_to_all(right, "col", split_axis=1, concat_axis=0, tiled=True),
+        check_the_rings(right, 1, 0),
     )
     return rows_update(
         lax.all_gather(left_part, "col", axis=1, tiled=True), right_cols, out_weight, out_bias

time: 119 us -> 126 us (1.059)
  the two profiles are of different devices: /device:TPU:9 before, /device:TPU:0 now
where the time goes in v1:
time: 126 us; the launch traced here: 125 us
  blocking collectives  31.1 us (25%)
  starting transfers between devices  30.1 us (24%)
  waiting for transfers between devices  24.8 us (20%)
  local copies, waits for them, and re-layouts  22 us (17%)
  matrix products  14.5 us (12%)
  other arithmetic  2.52 us (2%)
    all_gather x1, blocking collectives, on_device(): lax.all_gather(left_part, 'col', axis=1, tiled=True)  31.1 us
    ppermute x15, waiting for transfers between devices, check_the_rings(): lax.ppermute(b_now, axis_name='col', perm=[(no, (no + i) % local_part) fo...  24.8 us
    ppermute x15, starting transfers between devices, check_the_rings(): lax.ppermute(b_now, axis_name='col', perm=[(no, (no + i) % local_part) fo...  22.7 us
    dot_general x4, matrix products, tile_update(): jnp.einsum('sic,sje->ijce', left_rows, right_cols, preferred_element_type...  8.49 us
    all_to_all x1, starting transfers between devices, on_device(): lax.all_to_all(left, 'col', split_axis=1, concat_axis=0, tiled=True)  7.41 us
    reshape x4, local copies, waits for them, and re-layouts, tile_update(): flat = outer.astype(jnp.bfloat16).reshape(count * columns, width * width)  6.79 us
    dot_general x4, matrix products, tile_update(): jnp.dot(flat, out_weight, preferred_element_type=jnp.float32) + out_bias  5.98 us
    convert_element_type x4, local copies, waits for them, and re-layouts, tile_update(): flat = outer.astype(jnp.bfloat16).reshape(count * columns, width * width)  5.42 us
  transfers between devices with their start and end apart: 16, of which 7 were waited for; matrix products, arithmetic and copies ran while one was open for 4% of the time, Pallas kernels for 0%

profile of v1, /device:TPU:0, one launch (start us, length us, event | category | flops | bytes accessed | tf_op | source)
XLA Modules:
  0.0 125.4 jit_solution(15973454242592859153)
XLA Ops:
  0.0 1.0 copy.20
  1.7 7.4 %all-to-all-start = ((bf16[16,2,512]{2,1,0:T(2,128)(2,1)}), bf16[16,2,512]{2,1,0:T(2,128)(2,1)S(1)}, u32[]{:S(2)}, u32[]{:S(2)}) async-start(bf16[16,2,512]{2,1,0:T(2,128)(2,1)} %reshape.16), calls=%async_computation | async-start | bytes 65536 | tf_op jit(solution)/shard_map/all_to_all | solution.py:47
  9.2 2.5 %fusion.6 = bf16[16,1280,32]{1,2,0:T(8,128)(2,1)S(1)} fusion(s32[]{:T(128)S(6)} %select_n.24, bf16[16,1280,32]{1,2,0:T(8,128)(2,1)} %param.7), kind=kLoop, calls=%fused_computation.11 | loop fusion | flops 2621440 | bytes 2621444 | tf_op jit(solution)/shard_map/jit(_roll_dynamic)/concatenate | solution.py:10
  11.7 1.4 %fusion.7 = (bf16[16,80,32]{1,2,0:T(8,128)(2,1)S(1)}, bf16[16,80,32]{1,2,0:T(8,128)(2,1)S(1)}, bf16[16,80,32]{1,2,0:T(8,128)(2,1)S(1)}, bf16[16,80,32]{1,2,0:T(8...) fusion(bf16[16,1280,32]{1,2,0:T(8,128)(2,1)S(1)} %fusion.6), kind=kLoop, calls=%fused_computation.45 | loop fusion | bytes 2457600 | tf_op jit(solution)/shard_map/slice | solution.py:13
  13.1 4.4 %collective-permute-start = (bf16[16,80,32]{1,2,0:T(8,128)(2,1)}, bf16[16,80,32]{1,2,0:T(8,128)(2,1)S(1)}, u32[]{:S(2)}, u32[]{:S(2)}) collective-permute-start(bf16[16,80,32]{1,2,0:T(8,128)(2,1)} %get-tuple-element.70), channel_id=1, source_target_pairs={{0,15},{1,0},{2,1},{3,2},{4,3},{5,4},{6,5},{7,6},{8,7},{9,8},{10,9... | collective-permute-start | bytes 245768 | tf_op jit(solution)/shard_map/ppermute | solution.py:15
  19.2 31.1 %all_gather.3 = bf16[256,32,32]{0,2,1:T(8,128)(2,1)} all-gather(bf16[256,2,32]{0,2,1:T(8,128)(2,1)S(1)} %copy.16), channel_id=1, replica_groups=mesh['groups'=2,'col'=16] {'col'}, dimensions={1}, use_global_device_ids=true | all-gather | bytes 557056 | tf_op jit(solution)/shard_map/all_gather | solution.py:51
  50.4 2.9 %collective-permute-start.7 = (bf16[16,80,32]{1,2,0:T(8,128)(2,1)S(1)}, bf16[16,80,32]{1,2,0:T(8,128)(2,1)S(1)}, u32[]{:S(2)}, u32[]{:S(2)}) collective-permute-start(bf16[16,80,32]{1,2,0:T(8,128)(2,1)S(1)} %get-tuple-element.63), channel_id=1, source_target_pairs={{0,8},{1,9},{2,10},{3,11},{4,12},{5,13},{6,14},{7,15},{8,0},{9,1},... | collective-permute-start | bytes 245768 | tf_op jit(solution)/shard_map/ppermute | solution.py:15
  53.5 3.6 %collective-permute-start.9 = (bf16[16,80,32]{1,2,0:T(8,128)(2,1)S(1)}, bf16[16,80,32]{1,2,0:T(8,128)(2,1)S(1)}, u32[]{:S(2)}, u32[]{:S(2)}) collective-permute-start(bf16[16,80,32]{1,2,0:T(8,128)(2,1)S(1)} %get-tuple-element.61), channel_id=1, source_target_pairs={{0,6},{1,7},{2,8},{3,9},{4,10},{5,11},{6,12},{7,13},{8,14},{9,15},... | collective-permute-start | bytes 245768 | tf_op jit(solution)/shard_map/ppermute | solution.py:15
  58.7 10.2 %collective-permute-start.11 = (bf16[16,80,32]{1,2,0:T(8,128)(2,1)S(1)}, bf16[16,80,32]{1,2,0:T(8,128)(2,1)S(1)}, u32[]{:S(2)}, u32[]{:S(2)}) collective-permute-start(bf16[16,80,32]{1,2,0:T(8,128)(2,1)S(1)} %get-tuple-element.59), channel_id=1, source_target_pairs={{0,4},{1,5},{2,6},{3,7},{4,8},{5,9},{6,10},{7,11},{8,12},{9,13},{1... | collective-permute-start | bytes 245768 | tf_op jit(solution)/shard_map/ppermute | solution.py:15
  68.9 6.9 %collective-permute-done.7 = bf16[16,80,32]{1,2,0:T(8,128)(2,1)S(1)} collective-permute-done((bf16[16,80,32]{1,2,0:T(8,128)(2,1)S(1)}, bf16[16,80,32]{1,2,0:T(8,128)(2,1)S(1)}, u32[]{:S(2)}, u32[]{:S(2)}) %collective-permute-start.7) | collective-permute-done | bytes 81952 | tf_op jit(solution)/shard_map/ppermute | solution.py:15
  75.8 3.6 %collective-permute-done.8 = bf16[16,80,32]{1,2,0:T(8,128)(2,1)S(1)} collective-permute-done((bf16[16,80,32]{1,2,0:T(8,128)(2,1)S(1)}, bf16[16,80,32]{1,2,0:T(8,128)(2,1)S(1)}, u32[]{:S(2)}, u32[]{:S(2)}) %collective-permute-start.8) | collective-permute-done | bytes 81952 | tf_op jit(solution)/shard_map/ppermute | solution.py:15
  79.4 5.8 %collective-permute-done.9 = bf16[16,80,32]{1,2,0:T(8,128)(2,1)S(1)} collective-permute-done((bf16[16,80,32]{1,2,0:T(8,128)(2,1)S(1)}, bf16[16,80,32]{1,2,0:T(8,128)(2,1)S(1)}, u32[]{:S(2)}, u32[]{:S(2)}) %collective-permute-start.9) | collective-permute-done | bytes 81952 | tf_op jit(solution)/shard_map/ppermute | solution.py:15
  85.3 2.2 %collective-permute-done.10 = bf16[16,80,32]{1,2,0:T(8,128)(2,1)S(1)} collective-permute-done((bf16[16,80,32]{1,2,0:T(8,128)(2,1)S(1)}, bf16[16,80,32]{1,2,0:T(8,128)(2,1)S(1)}, u32[]{:S(2)}, u32[]{:S(2)}) %collective-permute-start.10) | collective-permute-done | bytes 81952 | tf_op jit(solution)/shard_map/ppermute | solution.py:15
  87.6 4.8 %collective-permute-done.14 = bf16[16,80,32]{1,2,0:T(8,128)(2,1)S(1)} collective-permute-done((bf16[16,80,32]{1,2,0:T(8,128)(2,1)S(1)}, bf16[16,80,32]{1,2,0:T(8,128)(2,1)S(1)}, u32[]{:S(2)}, u32[]{:S(2)}) %collective-permute-start.14) | collective-permute-done | bytes 81952 | tf_op jit(solution)/shard_map/ppermute | solution.py:15
  93.2 2.6 %copy.17 = bf16[256,80,32]{0,1,2:T(8,128)(2,1)} copy(bf16[256,80,32]{1,2,0:T(8,128)(2,1)S(1)} %constant_dynamic-slice_fusion) | data formatting | bytes 2621440 | tf_op jit(solution)/shard_map/while | solution.py:41
  95.9 29.5 %while.10 = (s32[]{:T(128)}, bf16[4,8,80,128]{3,2,1,0:T(8,128)(2,1)}, bf16[4,256,8,32]{1,3,2,0:T(8,128)(2,1)}, bf16[256,80,32]{0,1,2:T(8,128)(2,1)}, bf16[1024,1...) while((s32[]{:T(128)}, bf16[4,8,80,128]{3,2,1,0:T(8,128)(2,1)}, bf16[4,256,8,32]{1,3,2,0:T(8,128)(2,1)}, ...), condition=%wide.region_1.2_spmd, body=%wide.region_0.1_spmd.sunk | while | flops 504791040 | bytes 10061389 | solution.py:41
  95.9 2.1 %fusion.20 = bf16[8,80,32,32]{1,2,3,0:T(8,128)(2,1)S(1)} fusion(bf16[256,80,32]{0,1,2:T(8,128)(2,1)} %get-tuple-element.125, bf16[4,256,8,32]{1,3,2,0:T(8,128)(2,1)} %get-tuple-element.124, s32[]{:T(128)} %get-tuple-element.115), kind=kOutput, calls=%fused_computation.1.clone.1 | convolution fusion | flops 336855040 | bytes 2753024 | tf_op jit(solution)/shard_map/while/body/eval_jaxpr/sic,sje->ijce/dot_general | solution.py:30
  98.0 1.4 %copy.22 = bf16[8,80,32,32]{1,0,3,2:T(8,128)(2,1)S(1)} copy(bf16[8,80,32,32]{1,2,3,0:T(8,128)(2,1)S(1)} %fusion.20) | data formatting | bytes 2621440 | tf_op jit(solution)/shard_map/while/body/eval_jaxpr/convert_element_type | solution.py:33
  99.4 1.7 %reshape.19 = bf16[640,1024]{0,1:T(8,128)(2,1)S(1)} reshape(bf16[8,80,32,32]{1,0,3,2:T(8,128)(2,1)S(1)} %copy.22) | data formatting | bytes 2621440 | tf_op jit(solution)/shard_map/while/body/eval_jaxpr/reshape | solution.py:33
  101.1 1.5 %fusion.21 = bf16[640,128]{1,0:T(8,128)(2,1)S(1)} fusion(bf16[640,1024]{0,1:T(8,128)(2,1)S(1)} %reshape.19, bf16[1024,128]{1,0:T(8,128)(2,1)} %get-tuple-element.126, f32[128]{0:T(128)S(1)} %get-tuple-element.127), kind=kOutput, calls=%fused_computation.4.clone.1 | convolution fusion | flops 167936000 | bytes 1737216 | tf_op jit(solution)/shard_map/while/body/eval_jaxpr/dot_general | solution.py:34
  103.3 2.1 %fusion.20 = bf16[8,80,32,32]{1,2,3,0:T(8,128)(2,1)S(1)} fusion(bf16[256,80,32]{0,1,2:T(8,128)(2,1)} %get-tuple-element.125, bf16[4,256,8,32]{1,3,2,0:T(8,128)(2,1)} %get-tuple-element.124, s32[]{:T(128)} %get-tuple-element.115), kind=kOutput, calls=%fused_computation.1.clone.1 | convolution fusion | flops 336855040 | bytes 2753024 | tf_op jit(solution)/shard_map/while/body/eval_jaxpr/sic,sje->ijce/dot_general | solution.py:30
  105.4 1.4 %copy.22 = bf16[8,80,32,32]{1,0,3,2:T(8,128)(2,1)S(1)} copy(bf16[8,80,32,32]{1,2,3,0:T(8,128)(2,1)S(1)} %fusion.20) | data formatting | bytes 2621440 | tf_op jit(solution)/shard_map/while/body/eval_jaxpr/convert_element_type | solution.py:33
  106.8 1.7 %reshape.19 = bf16[640,1024]{0,1:T(8,128)(2,1)S(1)} reshape(bf16[8,80,32,32]{1,0,3,2:T(8,128)(2,1)S(1)} %copy.22) | data formatting | bytes 2621440 | tf_op jit(solution)/shard_map/while/body/eval_jaxpr/reshape | solution.py:33
  108.5 1.5 %fusion.21 = bf16[640,128]{1,0:T(8,128)(2,1)S(1)} fusion(bf16[640,1024]{0,1:T(8,128)(2,1)S(1)} %reshape.19, bf16[1024,128]{1,0:T(8,128)(2,1)} %get-tuple-element.126, f32[128]{0:T(128)S(1)} %get-tuple-element.127), kind=kOutput, calls=%fused_computation.4.clone.1 | convolution fusion | flops 167936000 | bytes 1737216 | tf_op jit(solution)/shard_map/while/body/eval_jaxpr/dot_general | solution.py:34
  110.7 2.1 %fusion.20 = bf16[8,80,32,32]{1,2,3,0:T(8,128)(2,1)S(1)} fusion(bf16[256,80,32]{0,1,2:T(8,128)(2,1)} %get-tuple-element.125, bf16[4,256,8,32]{1,3,2,0:T(8,128)(2,1)} %get-tuple-element.124, s32[]{:T(128)} %get-tuple-element.115), kind=kOutput, calls=%fused_computation.1.clone.1 | convolution fusion | flops 336855040 | bytes 2753024 | tf_op jit(solution)/shard_map/while/body/eval_jaxpr/sic,sje->ijce/dot_general | solution.py:30
  112.8 1.4 %copy.22 = bf16[8,80,32,32]{1,0,3,2:T(8,128)(2,1)S(1)} copy(bf16[8,80,32,32]{1,2,3,0:T(8,128)(2,1)S(1)} %fusion.20) | data formatting | bytes 2621440 | tf_op jit(solution)/shard_map/while/body/eval_jaxpr/convert_element_type | solution.py:33
  114.1 1.7 %reshape.19 = bf16[640,1024]{0,1:T(8,128)(2,1)S(1)} reshape(bf16[8,80,32,32]{1,0,3,2:T(8,128)(2,1)S(1)} %copy.22) | data formatting | bytes 2621440 | tf_op jit(solution)/shard_map/while/body/eval_jaxpr/reshape | solution.py:33
  115.8 1.5 %fusion.21 = bf16[640,128]{1,0:T(8,128)(2,1)S(1)} fusion(bf16[640,1024]{0,1:T(8,128)(2,1)S(1)} %reshape.19, bf16[1024,128]{1,0:T(8,128)(2,1)} %get-tuple-element.126, f32[128]{0:T(128)S(1)} %get-tuple-element.127), kind=kOutput, calls=%fused_computation.4.clone.1 | convolution fusion | flops 167936000 | bytes 1737216 | tf_op jit(solution)/shard_map/while/body/eval_jaxpr/dot_general | solution.py:34
  118.0 2.1 %fusion.20 = bf16[8,80,32,32]{1,2,3,0:T(8,128)(2,1)S(1)} fusion(bf16[256,80,32]{0,1,2:T(8,128)(2,1)} %get-tuple-element.125, bf16[4,256,8,32]{1,3,2,0:T(8,128)(2,1)} %get-tuple-element.124, s32[]{:T(128)} %get-tuple-element.115), kind=kOutput, calls=%fused_computation.1.clone.1 | convolution fusion | flops 336855040 | bytes 2753024 | tf_op jit(solution)/shard_map/while/body/eval_jaxpr/sic,sje->ijce/dot_general | solution.py:30
  120.2 1.4 %copy.22 = bf16[8,80,32,32]{1,0,3,2:T(8,128)(2,1)S(1)} copy(bf16[8,80,32,32]{1,2,3,0:T(8,128)(2,1)S(1)} %fusion.20) | data formatting | bytes 2621440 | tf_op jit(solution)/shard_map/while/body/eval_jaxpr/convert_element_type | solution.py:33
  121.5 1.7 %reshape.19 = bf16[640,1024]{0,1:T(8,128)(2,1)S(1)} reshape(bf16[8,80,32,32]{1,0,3,2:T(8,128)(2,1)S(1)} %copy.22) | data formatting | bytes 2621440 | tf_op jit(solution)/shard_map/while/body/eval_jaxpr/reshape | solution.py:33
  123.2 1.5 %fusion.21 = bf16[640,128]{1,0:T(8,128)(2,1)S(1)} fusion(bf16[640,1024]{0,1:T(8,128)(2,1)S(1)} %reshape.19, bf16[1024,128]{1,0:T(8,128)(2,1)} %get-tuple-element.126, f32[128]{0:T(128)S(1)} %get-tuple-element.127), kind=kOutput, calls=%fused_computation.4.clone.1 | convolution fusion | flops 167936000 | bytes 1737216 | tf_op jit(solution)/shard_map/while/body/eval_jaxpr/dot_general | solution.py:34
  (66 shorter events, 7.9 us)
Async XLA Ops:
  1.7 17.2 %all-to-all-start = ((bf16[16,2,512]{2,1,0:T(2,128)(2,1)}), bf16[16,2,512]{2,1,0:T(2,128)(2,1)S(1)}, u32[]{:S(2)}, u32[]{:S(2)}) async-start(bf16[16,2,512]{2,1,0:T(2,128)(2,1)} %reshape.16), calls=%async_computation | async-start | bytes 65536 | tf_op jit(solution)/shard_map/all_to_all | solution.py:47
  13.1 37.2 %collective-permute-start = (bf16[16,80,32]{1,2,0:T(8,128)(2,1)}, bf16[16,80,32]{1,2,0:T(8,128)(2,1)S(1)}, u32[]{:S(2)}, u32[]{:S(2)}) collective-permute-start(bf16[16,80,32]{1,2,0:T(8,128)(2,1)} %get-tuple-element.70), channel_id=1, source_target_pairs={{0,15},{1,0},{2,1},{3,2},{4,3},{5,4},{6,5},{7,6},{8,7},{9,8},{10,9... | collective-permute-start | bytes 245768 | tf_op jit(solution)/shard_map/ppermute | solution.py:15
  17.5 32.8 %collective-permute-start.1 = (bf16[16,80,32]{1,2,0:T(8,128)(2,1)}, bf16[16,80,32]{1,2,0:T(8,128)(2,1)S(1)}, u32[]{:S(2)}, u32[]{:S(2)}) collective-permute-start(bf16[16,80,32]{1,2,0:T(8,128)(2,1)} %get-tuple-element.69), channel_id=1, source_target_pairs={{0,14},{1,15},{2,0},{3,1},{4,2},{5,3},{6,4},{7,5},{8,6},{9,7},{10,... | collective-permute-start | bytes 245768 | tf_op jit(solution)/shard_map/ppermute | solution.py:15
  18.0 32.4 %collective-permute-start.2 = (bf16[16,80,32]{1,2,0:T(8,128)(2,1)}, bf16[16,80,32]{1,2,0:T(8,128)(2,1)S(1)}, u32[]{:S(2)}, u32[]{:S(2)}) collective-permute-start(bf16[16,80,32]{1,2,0:T(8,128)(2,1)} %get-tuple-element.68), channel_id=1, source_target_pairs={{0,13},{1,14},{2,15},{3,0},{4,1},{5,2},{6,3},{7,4},{8,5},{9,6},{10... | collective-permute-start | bytes 245768 | tf_op jit(solution)/shard_map/ppermute | solution.py:15
  18.1 35.2 %collective-permute-start.3 = (bf16[16,80,32]{1,2,0:T(8,128)(2,1)}, bf16[16,80,32]{1,2,0:T(8,128)(2,1)S(1)}, u32[]{:S(2)}, u32[]{:S(2)}) collective-permute-start(bf16[16,80,32]{1,2,0:T(8,128)(2,1)} %get-tuple-element.67), channel_id=1, source_target_pairs={{0,12},{1,13},{2,14},{3,15},{4,0},{5,1},{6,2},{7,3},{8,4},{9,5},{1... | collective-permute-start | bytes 245768 | tf_op jit(solution)/shard_map/ppermute | solution.py:15
  18.7 34.7 %collective-permute-start.4 = (bf16[16,80,32]{1,2,0:T(8,128)(2,1)}, bf16[16,80,32]{1,2,0:T(8,128)(2,1)S(1)}, u32[]{:S(2)}, u32[]{:S(2)}) collective-permute-start(bf16[16,80,32]{1,2,0:T(8,128)(2,1)} %get-tuple-element.66), channel_id=1, source_target_pairs={{0,11},{1,12},{2,13},{3,14},{4,15},{5,0},{6,1},{7,2},{8,3},{9,4},{... | collective-permute-start | bytes 245768 | tf_op jit(solution)/shard_map/ppermute | solution.py:15
  50.3 7.7 %collective-permute-start.5 = (bf16[16,80,32]{1,2,0:T(8,128)(2,1)S(1)}, bf16[16,80,32]{1,2,0:T(8,128)(2,1)S(1)}, u32[]{:S(2)}, u32[]{:S(2)}) collective-permute-start(bf16[16,80,32]{1,2,0:T(8,128)(2,1)S(1)} %get-tuple-element.65), channel_id=1, source_target_pairs={{0,10},{1,11},{2,12},{3,13},{4,14},{5,15},{6,0},{7,1},{8,2},{9,3},... | collective-permute-start | bytes 245768 | tf_op jit(solution)/shard_map/ppermute | solution.py:15
  50.3 8.4 %collective-permute-start.6 = (bf16[16,80,32]{1,2,0:T(8,128)(2,1)S(1)}, bf16[16,80,32]{1,2,0:T(8,128)(2,1)S(1)}, u32[]{:S(2)}, u32[]{:S(2)}) collective-permute-start(bf16[16,80,32]{1,2,0:T(8,128)(2,1)S(1)} %get-tuple-element.64), channel_id=1, source_target_pairs={{0,9},{1,10},{2,11},{3,12},{4,13},{5,14},{6,15},{7,0},{8,1},{9,2},... | collective-permute-start | bytes 245768 | tf_op jit(solution)/shard_map/ppermute | solution.py:15
  50.4 25.4 %collective-permute-start.7 = (bf16[16,80,32]{1,2,0:T(8,128)(2,1)S(1)}, bf16[16,80,32]{1,2,0:T(8,128)(2,1)S(1)}, u32[]{:S(2)}, u32[]{:S(2)}) collective-permute-start(bf16[16,80,32]{1,2,0:T(8,128)(2,1)S(1)} %get-tuple-element.63), channel_id=1, source_target_pairs={{0,8},{1,9},{2,10},{3,11},{4,12},{5,13},{6,14},{7,15},{8,0},{9,1},... | collective-permute-start | bytes 245768 | tf_op jit(solution)/shard_map/ppermute | solution.py:15
  53.4 26.0 %collective-permute-start.8 = (bf16[16,80,32]{1,2,0:T(8,128)(2,1)S(1)}, bf16[16,80,32]{1,2,0:T(8,128)(2,1)S(1)}, u32[]{:S(2)}, u32[]{:S(2)}) collective-permute-start(bf16[16,80,32]{1,2,0:T(8,128)(2,1)S(1)} %get-tuple-element.62), channel_id=1, source_target_pairs={{0,7},{1,8},{2,9},{3,10},{4,11},{5,12},{6,13},{7,14},{8,15},{9,0},... | collective-permute-start | bytes 245768 | tf_op jit(solution)/shard_map/ppermute | solution.py:15
  53.5 31.8 %collective-permute-start.9 = (bf16[16,80,32]{1,2,0:T(8,128)(2,1)S(1)}, bf16[16,80,32]{1,2,0:T(8,128)(2,1)S(1)}, u32[]{:S(2)}, u32[]{:S(2)}) collective-permute-start(bf16[16,80,32]{1,2,0:T(8,128)(2,1)S(1)} %get-tuple-element.61), channel_id=1, source_target_pairs={{0,6},{1,7},{2,8},{3,9},{4,10},{5,11},{6,12},{7,13},{8,14},{9,15},... | collective-permute-start | bytes 245768 | tf_op jit(solution)/shard_map/ppermute | solution.py:15
  57.9 29.5 %collective-permute-start.10 = (bf16[16,80,32]{1,2,0:T(8,128)(2,1)S(1)}, bf16[16,80,32]{1,2,0:T(8,128)(2,1)S(1)}, u32[]{:S(2)}, u32[]{:S(2)}) collective-permute-start(bf16[16,80,32]{1,2,0:T(8,128)(2,1)S(1)} %get-tuple-element.60), channel_id=1, source_target_pairs={{0,5},{1,6},{2,7},{3,8},{4,9},{5,10},{6,11},{7,12},{8,13},{9,14},{... | collective-permute-start | bytes 245768 | tf_op jit(solution)/shard_map/ppermute | solution.py:15
  58.7 28.7 %collective-permute-start.11 = (bf16[16,80,32]{1,2,0:T(8,128)(2,1)S(1)}, bf16[16,80,32]{1,2,0:T(8,128)(2,1)S(1)}, u32[]{:S(2)}, u32[]{:S(2)}) collective-permute-start(bf16[16,80,32]{1,2,0:T(8,128)(2,1)S(1)} %get-tuple-element.59), channel_id=1, source_target_pairs={{0,4},{1,5},{2,6},{3,7},{4,8},{5,9},{6,10},{7,11},{8,12},{9,13},{1... | collective-permute-start | bytes 245768 | tf_op jit(solution)/shard_map/ppermute | solution.py:15
  75.8 11.7 %collective-permute-start.12 = (bf16[16,80,32]{1,2,0:T(8,128)(2,1)S(1)}, bf16[16,80,32]{1,2,0:T(8,128)(2,1)S(1)}, u32[]{:S(2)}, u32[]{:S(2)}) collective-permute-start(bf16[16,80,32]{1,2,0:T(8,128)(2,1)S(1)} %get-tuple-element.58), channel_id=1, source_target_pairs={{0,3},{1,4},{2,5},{3,6},{4,7},{5,8},{6,9},{7,10},{8,11},{9,12},{10... | collective-permute-start | bytes 245768 | tf_op jit(solution)/shard_map/ppermute | solution.py:15
  79.4 8.1 %collective-permute-start.13 = (bf16[16,80,32]{1,2,0:T(8,128)(2,1)S(1)}, bf16[16,80,32]{1,2,0:T(8,128)(2,1)S(1)}, u32[]{:S(2)}, u32[]{:S(2)}) collective-permute-start(bf16[16,80,32]{1,2,0:T(8,128)(2,1)S(1)} %get-tuple-element.57), channel_id=1, source_target_pairs={{0,2},{1,3},{2,4},{3,5},{4,6},{5,7},{6,8},{7,9},{8,10},{9,11},{10,... | collective-permute-start | bytes 245768 | tf_op jit(solution)/shard_map/ppermute | solution.py:15
  85.2 7.1 %collective-permute-start.14 = (bf16[16,80,32]{1,2,0:T(8,128)(2,1)S(1)}, bf16[16,80,32]{1,2,0:T(8,128)(2,1)S(1)}, u32[]{:S(2)}, u32[]{:S(2)}) collective-permute-start(bf16[16,80,32]{1,2,0:T(8,128)(2,1)S(1)} %get-tuple-element.56), channel_id=1, source_target_pairs={{0,1},{1,2},{2,3},{3,4},{4,5},{5,6},{6,7},{7,8},{8,9},{9,10},{10,1... | collective-permute-start | bytes 245768 | tf_op jit(solution)/shard_map/ppermute | solution.py:15
  92.8 3.1 %copy-start = (f32[128]{0:T(128)S(1)}, f32[128]{0:T(128)}, u32[]{:S(2)}) copy-start(f32[128]{0:T(128)} %param.9) | copy-start | bytes 1540
